TPU v7x, 128 devices: a whole 4x4x4 slice. The times are simulated.
128 devices in a mesh: grp: 4 (over z), seq: 32 (over x, y, core).
Axes of the slice: x: 4, y: 4, z: 4, core: 2. Of those that a mesh axis runs over, the one named last changes fastest.
Arguments:
- latent: bfloat16 [4, 4096, 32, 256], P('grp', 'seq'), may hold values from -6 to 6
- up_key: bfloat16 [4, 128, 256], replicated, may hold values from -0.5 to 0.5
- up_value: bfloat16 [4, 128, 256], replicated, may hold values from -0.5 to 0.5
- queries: bfloat16 [8, 64, 128], replicated, may hold values from -240 to 240, as said below
- lengths: int32 [8], replicated, may hold values from 1 to 16384
- block_dest: int32 [4096], replicated, may hold values from 0 to 127, as said below
Outputs:
- decode_latent: bfloat16 [128, 4, 32, 32, 256], P(('grp', 'seq'))
- attended: float32 [8, 8192], replicated
Inputs may be any that keep to these rules, and one draw needn't show every extreme that they name: `block_dest`: each aligned run of 128 entries (the blocks of one seq index in the prefill layout) names every decode device exactly once. `queries`: the new token's query entries, real-valued.
All inputs are finite; a program needn't handle non-finite values.
Results may differ from a plain program's by a relative error of at most 0.001.
Values may be sent and summed in bfloat16 or wider, within the bound.
A program may use at most 64 MiB of HBM per device.

v0:
```python
import jax
import jax.numpy as jnp
from jax import lax
from jax.sharding import Mesh
from jax.sharding import PartitionSpec as P

SEQ = ("seq_0", "seq_1", "seq_2")
GRP_SEQ = ("grp", "seq_0", "seq_1", "seq_2")


def all_in_one(x, axis):
    leaves = jax.tree.leaves(x)
    turns = sorted(range(len(leaves)), key=lambda k: -leaves[k].size)
    width = (1, *leaves[turns[0]].shape)[-1]
    lines = [
        jnp.pad(leaves[k].reshape(-1), (0, -leaves[k].size % width)).reshape(-1, width)
        for k in turns
    ]
    both, at, found = (lax.all_gather(jnp.concatenate(lines), axis), 0, {})
    for k, line in zip(turns, lines):
        slab = both[:, at : at + len(line)].reshape(len(both), -1)
        found[k] = slab[:, : leaves[k].size].reshape(-1, *leaves[k].shape)
        at += len(line)
    numbers = iter(range(len(leaves)))
    return jax.tree.map(lambda _: found[next(numbers)], x)


def joined_all(x, axes, combine):
    for axis in axes:
        pieces = all_in_one(x, axis)
        x = jax.tree.map(lambda part: part[0], pieces)
        for k in range(1, lax.axis_size(axis)):
            x = combine(x, jax.tree.map(lambda part: part[k], pieces))
    return x


def combine(first, second):
    largest = jnp.maximum(first[0], second[0])
    factor_a = jnp.exp(first[0] - largest)
    factor_b = jnp.exp(second[0] - largest)
    totals = first[1] * factor_a + second[1] * factor_b
    accum = first[2] * factor_a[..., None] + second[2] * factor_b[..., None]
    return (largest, totals, accum)


def slot_info(global_ids, lengths, block_len, blk_seq, batch):
    seq_ids = global_ids // blk_seq
    starts = global_ids % blk_seq * block_len
    positions = starts[:, None] + jnp.arange(block_len, dtype=jnp.int32)[None, :]
    seq_hot = (seq_ids[:, None] == jnp.arange(batch, dtype=jnp.int32)[None, :]).astype(jnp.int32)
    slot_len = jnp.sum(seq_hot * lengths[None, :], axis=1)
    live = positions < slot_len[:, None]
    return (seq_hot, live)


def partials(cache, key_map, value_map, slot_query, live, seq_hot):
    rank = cache.shape[3] // 2
    head_dim = slot_query.shape[-1]
    scale = 1.0 / float(head_dim) ** 0.5
    highest = lax.Precision.HIGHEST
    key_lat = cache[..., :rank]
    value_lat = cache[..., rank:]
    keys = jnp.einsum("gstr,grkd->gstkd", key_lat, key_map, preferred_element_type=jnp.float32)
    scores = (
        jnp.einsum("gstkd,sgkjd->gskjt", keys, slot_query.astype(jnp.float32), precision=highest)
        * scale
    )
    live_wide = live[None, :, None, None, :]
    scores = jnp.where(live_wide, scores, -1e30)
    slot_max = jnp.max(scores, axis=-1)
    weights = jnp.where(live_wide, jnp.exp(scores - slot_max[..., None]), 0.0)
    slot_tot = jnp.sum(weights, axis=-1)
    values = jnp.einsum(
        "gstr,grkd->gstkd", value_lat, value_map, preferred_element_type=jnp.float32
    )
    slot_acc = jnp.einsum("gskjt,gstkd->gskjd", weights, values, precision=highest)
    hot_bool = seq_hot > 0
    hot_float = seq_hot.astype(jnp.float32)
    spread = jnp.where(hot_bool[None, :, None, None, :], slot_max[..., None], -1e30)
    seq_max = jnp.max(spread, axis=1)
    slot_seq_max = jnp.sum(
        jnp.where(hot_bool[None, :, None, None, :], seq_max[:, None], 0.0), axis=-1
    )
    factor = jnp.exp(slot_max - slot_seq_max)
    totals = jnp.einsum("gskj,sb->gkjb", slot_tot * factor, hot_float, precision=highest)
    accum = jnp.einsum(
        "gskjd,sb->gkjbd", slot_acc * factor[..., None], hot_float, precision=highest
    )
    return (seq_max, totals, accum)


def body(latent, up_key, up_value, queries, lengths, block_dest):
    groups = up_key.shape[0]
    dests = latent.shape[1]
    block_len = latent.shape[2]
    rank = latent.shape[3] // 2
    shards = block_dest.shape[0] // dests
    batch = queries.shape[0]
    q_heads = queries.shape[1]
    head_dim = queries.shape[2]
    per_group = up_key.shape[2] // head_dim
    per_kv = q_heads // (groups * per_group)
    blk_seq = block_dest.shape[0] // batch
    own_shard = lax.axis_index(SEQ)
    own_dests = lax.dynamic_slice_in_dim(block_dest, own_shard * dests, dests)
    source_order = (
        jnp.zeros((dests,), jnp.int32).at[own_dests].set(jnp.arange(dests, dtype=jnp.int32))
    )
    outgoing = latent[0][source_order]
    received = lax.all_to_all(outgoing, GRP_SEQ, split_axis=0, concat_axis=0, tiled=True)
    received = received.reshape(groups, shards, block_len, 2 * rank)
    decode_latent = received[None]
    key_map = up_key.reshape(groups, rank, per_group, head_dim)
    value_map = up_value.reshape(groups, rank, per_group, head_dim)
    query_rows = queries.reshape(batch, q_heads * head_dim)
    own_group = lax.axis_index("grp")
    slots = latent.shape[1]
    global_ids = own_shard * slots + jnp.arange(slots, dtype=jnp.int32)
    seq_hot, live = slot_info(global_ids, lengths, block_len, blk_seq, batch)
    picked = jnp.dot(seq_hot.astype(jnp.bfloat16), query_rows, preferred_element_type=jnp.float32)
    slot_query = picked.astype(jnp.bfloat16).reshape(slots, groups, per_group, per_kv, head_dim)
    group_query = lax.dynamic_slice_in_dim(slot_query, own_group, 1, 1)
    group_key = lax.dynamic_slice_in_dim(key_map, own_group, 1, 0)
    group_value = lax.dynamic_slice_in_dim(value_map, own_group, 1, 0)
    local = partials(latent, group_key, group_value, group_query, live, seq_hot)
    merged = joined_all(local, SEQ, combine)
    part_result = merged[2] / merged[1][..., None]
    result = lax.all_gather(part_result, "grp", axis=0, tiled=True)
    attended = jnp.transpose(result, (3, 0, 1, 2, 4)).reshape(batch, q_heads * head_dim)
    return (decode_latent, attended)


def solution(mesh):
    finer = Mesh(
        mesh.devices.reshape(mesh.shape["grp"], 4, 4, 2), ("grp", "seq_0", "seq_1", "seq_2")
    )
    in_specs = (P("grp", SEQ, None, None), P(), P(), P(), P(), P())
    out_specs = (P(GRP_SEQ, None, None, None, None), P())
    return jax.shard_map(body, mesh=finer, in_specs=in_specs, out_specs=out_specs, check_vma=False)
```

profile of v0, /device:TPU:0, one launch (start us, length us, event | category | flops | bytes accessed | tf_op | source)
XLA Modules:
  0.0 82.2 jit_solution(2277621008148799493)
XLA Ops:
  0.6 0.8 compare_select_fusion.1
  1.4 1.0 %scatter_custom_fusion = s32[128]{0:T(128)S(1)} fusion(s32[128]{0:T(128)S(1)} %compare_select_fusion.1, s32[128]{0:T(128)S(1)} %iota.27, s32[]{:T(128)} %constant.26.clone.1), kind=kCustom, calls=%fused_computation.172 | custom fusion | bytes 516 | tf_op jit(solution)/shard_map/scatter | solution.py:107
  2.4 3.6 %gather_fusion = bf16[128,32,256]{2,1,0:T(8,128)(2,1)} fusion(bf16[128,32,256]{2,1,0:T(8,128)(2,1)} %bitcast.358, s32[1024]{0:T(1024)S(1)} %pad_clamp_fusion), kind=kCustom, calls=%fused_computation | custom fusion | bytes 4194816 | tf_op jit(solution)/shard_map/gather | solution.py:109
  6.0 0.0 copy-start.4
  6.0 0.0 copy-start.1
  6.0 0.0 copy-start.2
  6.0 0.0 copy-start
  6.0 11.7 %all-to-all-start = ((bf16[128,32,256]{2,1,0:T(8,128)(2,1)}), bf16[128,32,256]{2,1,0:T(8,128)(2,1)}, u32[]{:S(2)}, u32[]{:S(2)}) async-start(bf16[128,32,256]{2,1,0:T(8,128)(2,1)} %gather_fusion), calls=%async_computation | async-start | bytes 4194304 | tf_op jit(solution)/shard_map/all_to_all | solution.py:110
  17.8 0.0 copy-done.4
  17.8 0.1 select_reduce_fusion.2
  17.9 0.0 copy-done.1
  17.9 0.1 reshape.1159
  17.9 0.0 copy-done.2
  17.9 0.1 reshape.1162
  18.0 0.1 constant_dynamic-slice_fusion
  18.1 0.0 copy-done
  18.1 0.0 copy-start.3
  18.1 0.7 fusion.14
  18.8 0.2 copy-done.3
  19.0 0.7 fusion.4
  19.8 0.6 copy.35
  20.4 0.1 add_compare_fusion
  20.5 3.6 %fusion.102 = (f32[128,2,8]{2,1,0:T(2,128)S(1)}, f32[128,2,8,32]{3,2,1,0:T(8,128)S(1)}) fusion(f32[2,128,128,32]{1,3,0,2:T(8,128)S(1)} %fusion.14, bf16[128,4,2,8,128]{4,3,2,1,0:T(8,128)(2,1)S(1)} %bitcast.359, s32[]{:T(128)S(6)} %select_n.72, pred[128,32]{1,0:T(8,128)(4,1)S(1)} %add_compare_fusion), kind=kOutput, calls=%fused_computation.176 | convolution fusion | flops 100857856 | bytes 5005316 | tf_op jit(solution)/shard_map/gstkd,sgkjd->gskjt/dot_general | solution.py:65
  24.2 0.1 copy.25
  24.2 0.1 select_reduce_fusion.1
  24.3 0.1 select_reduce_fusion
  24.4 0.1 reshape.1166
  24.5 0.1 copy.26
  24.7 0.7 convolution_bitcast_fusion
  25.4 0.8 fusion.21
  26.2 3.7 %fusion.5 = f32[128,2,8,128]{3,2,1,0:T(8,128)S(1)} fusion(f32[128,32,2,128]{3,1,0,2:T(8,128)S(1)} %convolution_bitcast_fusion, f32[128,2,8,32]{3,2,1,0:T(8,128)S(1)} %get-tuple-element.30, f32[128,2,8]{2,1,0:T(2,128)S(1)} %copy.26, f32[128,2,8]{2,1,0:T(2,128)S(1)} %get-tuple-element.29, pred[128,32]{1,0:T(8,128)(4,1)S(1)} %add_compare_fusion), kind=kOutput, calls=%fused_computation.9 | convolution fusion | flops 101056512 | bytes 5525504 | tf_op jit(solution)/shard_map/gskjt,gstkd->gskjd/dot_general | solution.py:76
  29.9 0.9 %fusion.17 = f32[8,2,8,128]{3,0,2,1:T(8,128)S(1)} fusion(f32[128,2,8,128]{3,2,1,0:T(8,128)S(1)} %fusion.5, s32[128]{0:T(128)S(1)} %get-tuple-element.31), kind=kOutput, calls=%fused_computation.15 | convolution fusion | flops 25168896 | bytes 1114624 | tf_op jit(solution)/shard_map/gskjd,sb->gkjbd/dot_general | solution.py:86
  30.7 0.1 copy.28
  30.8 0.1 fusion.49
  30.9 0.1 reshape.1167
  31.1 18.3 %all-gather.3 = f32[4,130,128]{2,1,0:T(8,128)S(1)} all-gather(f32[1,130,128]{2,1,0:T(8,128)S(1)} %maximum_bitcast_fusion), channel_id=2, replica_groups=mesh['grp'=4,'seq_0'=4,'seq_1'=4,'seq_2'=2] {'seq_0'}, dimensions={0}, use_global_device_ids=true | all-gather | bytes 332800 | tf_op jit(solution)/shard_map/all_gather | solution.py:19
  49.4 0.2 fusion.39
  49.6 12.7 %all-gather.4 = f32[4,130,128]{2,1,0:T(8,128)S(1)} all-gather(f32[1,130,128]{2,1,0:T(8,128)S(1)} %maximum_bitcast_fusion.1), channel_id=3, replica_groups=mesh['grp'=4,'seq_0'=4,'seq_1'=4,'seq_2'=2] {'seq_1'}, dimensions={0}, use_global_device_ids=true | all-gather | bytes 332800 | tf_op jit(solution)/shard_map/all_gather | solution.py:19
  62.4 0.2 fusion.30
  62.6 1.9 %all-gather.5 = f32[2,130,128]{2,1,0:T(8,128)S(1)} all-gather(f32[1,130,128]{2,1,0:T(8,128)S(1)} %maximum_bitcast_fusion.2), channel_id=4, replica_groups=mesh['grp'=4,'seq_0'=4,'seq_1'=4,'seq_2'=2] {'seq_2'}, dimensions={0}, use_global_device_ids=true | all-gather | bytes 199680 | tf_op jit(solution)/shard_map/all_gather | solution.py:19
  64.5 0.1 squeeze.143
  64.6 0.1 squeeze.144
  64.7 0.1 squeeze.146
  64.8 0.1 squeeze.147
  64.9 0.1 add_divide_fusion
  65.0 13.4 %all_gather.27 = f32[4,2,8,8,128]{4,3,2,1,0:T(8,128)S(1)} all-gather(f32[1,2,8,8,128]{4,3,2,1,0:T(8,128)S(1)} %add_divide_fusion), channel_id=1, replica_groups=mesh['grp'=4,'seq_0'=4,'seq_1'=4,'seq_2'=2] {'grp'}, dimensions={0}, use_global_device_ids=true | all-gather | bytes 327680 | tf_op jit(solution)/shard_map/all_gather | solution.py:128
  78.4 0.0 all-to-all-done
  78.4 3.1 %copy.52 = bf16[1,4,32,32,256]{4,3,2,1,0:T(8,128)(2,1)} copy(bf16[1,4,32,32,256]{4,3,2,1,0:T(8,128)(2,1)} %bitcast.1) | data formatting | bytes 4194304
  81.5 0.7 copy.53
  (18 shorter events, 0.2 us)
Async XLA Ops:
  6.0 11.8 %copy-start.4 = (s32[8]{0:T(128)S(1)}, s32[8]{0:T(128)}, u32[]{:S(2)}) copy-start(s32[8]{0:T(128)} %param.10) | copy-start | bytes 100
  6.0 11.9 %copy-start.1 = (bf16[4,128,256]{2,1,0:T(8,128)(2,1)S(1)}, bf16[4,128,256]{2,1,0:T(8,128)(2,1)}, u32[]{:S(2)}) copy-start(bf16[4,128,256]{2,1,0:T(8,128)(2,1)} %param.7) | copy-start | bytes 786436
  6.0 11.9 %copy-start.2 = (bf16[4,128,256]{2,1,0:T(8,128)(2,1)S(1)}, bf16[4,128,256]{2,1,0:T(8,128)(2,1)}, u32[]{:S(2)}) copy-start(bf16[4,128,256]{2,1,0:T(8,128)(2,1)} %param.8) | copy-start | bytes 786436
  6.0 12.1 %copy-start = (bf16[1,128,32,256]{3,2,1,0:T(8,128)(2,1)S(1)}, bf16[1,128,32,256]{3,2,1,0:T(8,128)(2,1)}, u32[]{:S(2)}) copy-start(bf16[1,128,32,256]{3,2,1,0:T(8,128)(2,1)} %param.6) | copy-start | bytes 6291460
  6.0 72.4 %all-to-all-start = ((bf16[128,32,256]{2,1,0:T(8,128)(2,1)}), bf16[128,32,256]{2,1,0:T(8,128)(2,1)}, u32[]{:S(2)}, u32[]{:S(2)}) async-start(bf16[128,32,256]{2,1,0:T(8,128)(2,1)} %gather_fusion), calls=%async_computation | async-start | bytes 4194304 | tf_op jit(solution)/shard_map/all_to_all | solution.py:110
  18.1 0.9 %copy-start.3 = (bf16[8,64,128]{2,1,0:T(8,128)(2,1)S(1)}, bf16[8,64,128]{2,1,0:T(8,128)(2,1)}, u32[]{:S(2)}) copy-start(bf16[8,64,128]{2,1,0:T(8,128)(2,1)} %param.9) | copy-start | bytes 393220
where the time goes:
time: 82.5 us; the launch traced here: 82.2 us
  blocking collectives  46.3 us (56%)
  starting transfers between devices  11.7 us (14%)
  matrix products  10.4 us (13%)
  local copies, waits for them, and re-layouts  10.2 us (12%)
  other arithmetic  2.58 us (3%)
  between operations  0.89 us (1%)
    all_gather x3, blocking collectives, all_in_one(): both, at, found = (lax.all_gather(jnp.concatenate(lines), axis), 0, {})  32.9 us
    all_gather x1, blocking collectives, body(): result = lax.all_gather(part_result, 'grp', axis=0, tiled=True)  13.4 us
    all_to_all x1, starting transfers between devices, body(): lax.all_to_all(outgoing, GRP_SEQ, split_axis=0, concat_axis=0, tiled=True)  11.7 us
    unnamed x13, local copies, waits for them, and re-layouts  4.61 us
    dot_general x1, matrix products, partials(): jnp.einsum('gskjt,gstkd->gskjd', weights, values, precision=highest)  3.68 us
    dot_general x1, matrix products, partials(): jnp.einsum('gstkd,sgkjd->gskjt', keys, slot_query.astype(jnp.float32), pr...  3.63 us
    gather x1, local copies, waits for them, and re-layouts, body(): outgoing = latent[0][source_order]  3.59 us
  transfers between devices with their start and end apart: 1, of which 0 were waited for; matrix products, arithmetic and copies ran while one was open for 17% of the time, Pallas kernels for 0%

commit v1 on v0

--- a/solution.py
+++ b/solution.py
@@ -3,6 +3,7 @@
 from jax import lax
 from jax.sharding import Mesh
 from jax.sharding import PartitionSpec as P
+from jax.lax import all_to_all, psum
 
 SEQ = ("seq_0", "seq_1", "seq_2")
 GRP_SEQ = ("grp", "seq_0", "seq_1", "seq_2")
@@ -125,7 +126,9 @@
     local = partials(latent, group_key, group_value, group_query, live, seq_hot)
     merged = joined_all(local, SEQ, combine)
     part_result = merged[2] / merged[1][..., None]
-    result = lax.all_gather(part_result, "grp", axis=0, tiled=True)
+    result = jnp.concatenate(
+        all_to_all(jnp.stack([part_result for _ in range(psum(1, "grp"))], 0), "grp", 0, 0), 0
+    )
     attended = jnp.transpose(result, (3, 0, 1, 2, 4)).reshape(batch, q_heads * head_dim)
     return (decode_latent, attended)
 

time: 82.5 us -> 103 us (1.25)
  waiting for transfers between devices: 0.01 us -> 33.6 us
  blocking collectives: 46.3 us -> 27.6 us
  matrix products: 10.4 us -> 13 us
  other arithmetic: 2.58 us -> 3.88 us
    all_to_all x1, waiting for transfers between devices: 0.01 us -> 30.3 us  [body(): lax.all_to_all(outgoing, GRP_SEQ, split_axis=0, concat_axis=0, tiled=True)]
    all_gather x1 -> x0, blocking collectives: 13.4 us -> none  [body(): result = lax.all_gather(part_result, 'grp', axis=0, tiled=True)]
    all_gather x3, blocking collectives: 32.9 us -> 27.6 us  [all_in_one(): both, at, found = (lax.all_gather(jnp.concatenate(lines), axis), 0, {})]
    all_to_all x0 -> x1, starting transfers between devices: none -> 5.3 us  [body(): all_to_all(jnp.stack([part_result for _ in range(psum(1, 'grp'))], 0), 'g...]
    all_to_all x1, starting transfers between devices: 11.7 us -> 6.85 us  [body(): lax.all_to_all(outgoing, GRP_SEQ, split_axis=0, concat_axis=0, tiled=True)]
    all_to_all x0 -> x1, waiting for transfers between devices: none -> 3.22 us  [body(): all_to_all(jnp.stack([part_result for _ in range(psum(1, 'grp'))], 0), 'g...]
    gather x1, local copies, waits for them, and re-layouts: 3.59 us -> 2 us  [body(): outgoing = latent[0][source_order]]
    unnamed x13 -> x11, local copies, waits for them, and re-layouts: 4.61 us -> 3.96 us
  transfers between devices with their start and end apart: 1 -> 2, of which waited for: 0 -> 2; matrix products, arithmetic and copies ran while one was open for 17% -> 4% of each run, Pallas kernels for 0% -> 0%
where the time goes in v1:
time: 103 us; the launch traced here: 102 us
  waiting for transfers between devices  33.6 us (33%)
  blocking collectives  27.6 us (27%)
  matrix products  13 us (13%)
  starting transfers between devices  12.2 us (12%)
  local copies, waits for them, and re-layouts  11.1 us (11%)
  other arithmetic  3.88 us (4%)
    all_to_all x1, waiting for transfers between devices, body(): lax.all_to_all(outgoing, GRP_SEQ, split_axis=0, concat_axis=0, tiled=True)  30.3 us
    all_gather x3, blocking collectives, all_in_one(): both, at, found = (lax.all_gather(jnp.concatenate(lines), axis), 0, {})  27.6 us
    all_to_all x1, starting transfers between devices, body(): lax.all_to_all(outgoing, GRP_SEQ, split_axis=0, concat_axis=0, tiled=True)  6.85 us
    all_to_all x1, starting transfers between devices, body(): all_to_all(jnp.stack([part_result for _ in range(psum(1, 'grp'))], 0), 'g...  5.3 us
    dot_general x1, matrix products, partials(): jnp.einsum('gstkd,sgkjd->gskjt', keys, slot_query.astype(jnp.float32), pr...  4.59 us
    unnamed x11, local copies, waits for them, and re-layouts  3.96 us
    dot_general x1, matrix products, partials(): jnp.einsum('gskjt,gstkd->gskjd', weights, values, precision=highest)  3.68 us
    all_to_all x1, waiting for transfers between devices, body(): all_to_all(jnp.stack([part_result for _ in range(psum(1, 'grp'))], 0), 'g...  3.22 us
  transfers between devices with their start and end apart: 2, of which 2 were waited for; matrix products, arithmetic and copies ran while one was open for 4% of the time, Pallas kernels for 0%

profile of v1, /device:TPU:0, one launch (start us, length us, event | category | flops | bytes accessed | tf_op | source)
XLA Modules:
  0.0 102.2 jit_solution(5024506107533336421)
XLA Ops:
  0.7 0.0 copy-start.2
  0.7 0.7 select_reduce_fusion.2
  1.4 1.0 reshape.1154
  2.4 1.0 reshape.1157
  3.5 0.0 copy-done.2
  3.5 1.7 %fusion.4 = bf16[16,8,64,128]{3,1,2,0:T(8,128)(2,1)S(1)} fusion(bf16[1,8,64,128]{3,2,1,0:T(8,128)(2,1)} %bitcast.367, s32[128]{0:T(128)S(1)} %get-tuple-element.31), kind=kOutput, calls=%fused_computation.8 | convolution fusion | flops 17828864 | bytes 2228736 | tf_op jit(solution)/shard_map/dot_general | solution.py:121
  5.1 0.0 copy-start
  5.1 1.9 %copy.35 = bf16[16,8,64,128]{3,2,1,0:T(8,128)(2,1)} copy(bf16[16,8,64,128]{3,1,2,0:T(8,128)(2,1)S(1)} %fusion.4) | data formatting | bytes 4194304
  7.1 0.1 add_compare_fusion
  7.2 0.1 constant_dynamic-slice_fusion
  7.3 0.0 copy-done
  7.3 0.7 fusion.14
  8.0 4.6 %fusion.102 = (f32[128,2,8]{2,1,0:T(2,128)S(1)}, f32[128,2,8,32]{3,2,1,0:T(8,128)S(1)}) fusion(f32[2,128,128,32]{1,3,0,2:T(8,128)S(1)} %fusion.14, bf16[128,4,2,8,128]{4,3,2,1,0:T(8,128)(2,1)} %bitcast.362, s32[]{:T(128)S(6)} %select_n.72, pred[128,32]{1,0:T(8,128)(4,1)S(1)} %add_compare_fusion), kind=kOutput, calls=%fused_computation.176 | convolution fusion | flops 100857856 | bytes 4993028 | tf_op jit(solution)/shard_map/gstkd,sgkjd->gskjt/dot_general | solution.py:66
  12.6 0.1 copy.25
  12.6 0.1 select_reduce_fusion.1
  12.7 0.1 select_reduce_fusion
  12.8 0.6 reshape.1161
  13.5 0.0 copy-start.1
  13.5 0.1 copy.26
  13.6 0.7 convolution_bitcast_fusion
  14.3 0.0 copy-done.1
  14.3 0.8 fusion.21
  15.1 0.0 copy-start.3
  15.1 3.7 %fusion.5 = f32[128,2,8,128]{3,2,1,0:T(8,128)S(1)} fusion(f32[128,32,2,128]{3,1,0,2:T(8,128)S(1)} %convolution_bitcast_fusion, f32[128,2,8,32]{3,2,1,0:T(8,128)S(1)} %get-tuple-element.30, f32[128,2,8]{2,1,0:T(2,128)S(1)} %copy.26, f32[128,2,8]{2,1,0:T(2,128)S(1)} %get-tuple-element.29, pred[128,32]{1,0:T(8,128)(4,1)S(1)} %add_compare_fusion), kind=kOutput, calls=%fused_computation.9 | convolution fusion | flops 101056512 | bytes 5525504 | tf_op jit(solution)/shard_map/gskjt,gstkd->gskjd/dot_general | solution.py:77
  18.8 0.0 copy-done.3
  18.8 0.9 fusion.17
  19.7 0.1 copy.28
  19.7 0.8 fusion.49
  20.6 0.1 reshape.1162
  20.7 0.7 maximum_bitcast_fusion
  21.4 12.7 %all-gather.3 = f32[4,130,128]{2,1,0:T(8,128)S(1)} all-gather(f32[1,130,128]{2,1,0:T(8,128)S(1)} %maximum_bitcast_fusion), channel_id=2, replica_groups=mesh['grp'=4,'seq_0'=4,'seq_1'=4,'seq_2'=2] {'seq_0'}, dimensions={0}, use_global_device_ids=true | all-gather | bytes 332800 | tf_op jit(solution)/shard_map/all_gather | solution.py:20
  34.1 0.2 fusion.39
  34.3 12.9 %all-gather.4 = f32[4,130,128]{2,1,0:T(8,128)S(1)} all-gather(f32[1,130,128]{2,1,0:T(8,128)S(1)} %maximum_bitcast_fusion.1), channel_id=3, replica_groups=mesh['grp'=4,'seq_0'=4,'seq_1'=4,'seq_2'=2] {'seq_1'}, dimensions={0}, use_global_device_ids=true | all-gather | bytes 332800 | tf_op jit(solution)/shard_map/all_gather | solution.py:20
  47.3 0.2 fusion.30
  47.5 1.9 %all-gather.5 = f32[2,130,128]{2,1,0:T(8,128)S(1)} all-gather(f32[1,130,128]{2,1,0:T(8,128)S(1)} %maximum_bitcast_fusion.2), channel_id=4, replica_groups=mesh['grp'=4,'seq_0'=4,'seq_1'=4,'seq_2'=2] {'seq_2'}, dimensions={0}, use_global_device_ids=true | all-gather | bytes 199680 | tf_op jit(solution)/shard_map/all_gather | solution.py:20
  49.4 0.1 squeeze.143
  49.5 0.1 squeeze.144
  49.6 0.1 squeeze.146
  49.7 0.1 squeeze.147
  49.8 0.1 add_divide_fusion
  49.9 0.7 stack.2
  50.6 5.3 %all-to-all-start.1 = ((f32[4,1,2,8,8,128]{5,4,3,2,1,0:T(8,128)}), f32[4,1,2,8,8,128]{5,4,3,2,1,0:T(8,128)S(1)}, u32[]{:S(2)}, u32[]{:S(2)}) async-start(f32[4,1,2,8,8,128]{5,4,3,2,1,0:T(8,128)} %stack.2), calls=%async_computation.1 | async-start | bytes 524288 | tf_op jit(solution)/shard_map/all_to_all | solution.py:130
  56.0 0.8 compare_select_fusion.1
  56.7 1.0 scatter_custom_fusion
  57.7 2.0 %gather_fusion = bf16[128,32,256]{2,1,0:T(8,128)(2,1)} fusion(bf16[128,32,256]{2,1,0:T(8,128)(2,1)S(1)} %bitcast.360, s32[1024]{0:T(1024)S(1)} %pad_clamp_fusion), kind=kCustom, calls=%fused_computation | custom fusion | bytes 4194816 | tf_op jit(solution)/shard_map/gather | solution.py:110
  59.7 3.2 %all-to-all-done.1 = f32[4,1,2,8,8,128]{5,4,3,2,1,0:T(8,128)S(1)} async-done(((f32[4,1,2,8,8,128]{5,4,3,2,1,0:T(8,128)}), f32[4,1,2,8,8,128]{5,4,3,2,1,0:T(8,128)S(1)}, u32[]{:S(2)}, u32[]{:S(2)}) %all-to-all-start.1) | async-done | bytes 262176 | tf_op jit(solution)/shard_map/all_to_all | solution.py:130
  62.9 6.9 %all-to-all-start = ((bf16[128,32,256]{2,1,0:T(8,128)(2,1)}), bf16[128,32,256]{2,1,0:T(8,128)(2,1)S(1)}, u32[]{:S(2)}, u32[]{:S(2)}) async-start(bf16[128,32,256]{2,1,0:T(8,128)(2,1)} %gather_fusion), calls=%async_computation | async-start | bytes 4194304 | tf_op jit(solution)/shard_map/all_to_all | solution.py:111
  69.8 30.3 %all-to-all-done = bf16[128,32,256]{2,1,0:T(8,128)(2,1)S(1)} async-done(((bf16[128,32,256]{2,1,0:T(8,128)(2,1)}), bf16[128,32,256]{2,1,0:T(8,128)(2,1)S(1)}, u32[]{:S(2)}, u32[]{:S(2)}) %all-to-all-start) | async-done | bytes 2097184 | tf_op jit(solution)/shard_map/all_to_all | solution.py:111
  100.1 1.3 %copy.52 = bf16[1,4,32,32,256]{4,3,2,1,0:T(8,128)(2,1)} copy(bf16[1,4,32,32,256]{4,3,2,1,0:T(8,128)(2,1)S(1)} %bitcast.361) | data formatting | bytes 4194304
  101.5 0.7 copy.53
  (17 shorter events, 0.2 us)
Async XLA Ops:
  0.7 2.8 %copy-start.2 = (s32[128]{0:T(128)}, s32[128]{0:T(128)S(1)}, u32[]{:S(2)}) copy-start(s32[128]{0:T(128)S(1)} %get-tuple-element.31) | copy-start | bytes 1540
  5.1 2.1 %copy-start = (bf16[1,128,32,256]{3,2,1,0:T(8,128)(2,1)S(1)}, bf16[1,128,32,256]{3,2,1,0:T(8,128)(2,1)}, u32[]{:S(2)}) copy-start(bf16[1,128,32,256]{3,2,1,0:T(8,128)(2,1)} %param.6) | copy-start | bytes 6291460
  13.5 0.9 copy-start.1
  15.1 3.7 %copy-start.3 = (s32[128]{0:T(128)S(1)}, s32[128]{0:T(128)}, u32[]{:S(2)}) copy-start(s32[128]{0:T(128)} %copy-done.2) | copy-start | bytes 1540
  50.6 12.3 %all-to-all-start.1 = ((f32[4,1,2,8,8,128]{5,4,3,2,1,0:T(8,128)}), f32[4,1,2,8,8,128]{5,4,3,2,1,0:T(8,128)S(1)}, u32[]{:S(2)}, u32[]{:S(2)}) async-start(f32[4,1,2,8,8,128]{5,4,3,2,1,0:T(8,128)} %stack.2), calls=%async_computation.1 | async-start | bytes 524288 | tf_op jit(solution)/shard_map/all_to_all | solution.py:130
  62.9 37.2 %all-to-all-start = ((bf16[128,32,256]{2,1,0:T(8,128)(2,1)}), bf16[128,32,256]{2,1,0:T(8,128)(2,1)S(1)}, u32[]{:S(2)}, u32[]{:S(2)}) async-start(bf16[128,32,256]{2,1,0:T(8,128)(2,1)} %gather_fusion), calls=%async_computation | async-start | bytes 4194304 | tf_op jit(solution)/shard_map/all_to_all | solution.py:111
